TPU v7x, 32 devices: a whole 2x2x4 slice. The times are simulated.
32 devices in a mesh: dom: 8 (over z, x), feat: 4 (over y, core).
Axes of the slice: x: 2, y: 2, z: 4, core: 2. Of those that a mesh axis runs over, the one named last changes fastest.
Arguments:
- grid_feat: bfloat16 [16384, 512], P(('dom', 'feat')), may hold values from -6 to 6
- mesh_feat: bfloat16 [1280, 512], P(('dom', 'feat')), may hold values from -6 to 6
- w_grid: bfloat16 [512, 512], P('feat'), may hold values from -0.25 to 0.25
- w_mesh: bfloat16 [512, 512], P('feat'), may hold values from -0.25 to 0.25
- w_enc2: bfloat16 [512, 512], P('feat'), may hold values from -0.25 to 0.25
- w_src: bfloat16 [512, 512], P('feat'), may hold values from -0.25 to 0.25
- w_dst: bfloat16 [512, 512], P('feat'), may hold values from -0.25 to 0.25
- w_proc2: bfloat16 [512, 512], P('feat'), may hold values from -0.25 to 0.25
- enc_send: int32 [256, 2], P(('dom', 'feat')), may hold values from -1 to 511, as said below
- enc_dst: int32 [256, 2], P(('dom', 'feat')), may hold values from -1 to 159, as said below
- hal_send: int32 [64, 4], P('dom'), may hold values from -1 to 159, as said below
- proc_src: int32 [5120], P(('dom', 'feat')), may hold values from 0 to 191, as said below
- proc_dst: int32 [5120], P(('dom', 'feat')), may hold values from 0 to 159
- cotangent: bfloat16 [1280, 512], P(('dom', 'feat')), may hold values from -6 to 6
Outputs:
- out: bfloat16 [1280, 512], P(('dom', 'feat'))
- g_grid: bfloat16 [16384, 512], P(('dom', 'feat'))
- g_mesh: bfloat16 [1280, 512], P(('dom', 'feat'))
- g_wgrid: float32 [512, 512], P('feat')
- g_wmesh: float32 [512, 512], P('feat')
- g_wenc2: float32 [512, 512], P('feat')
- g_wsrc: float32 [512, 512], P('feat')
- g_wdst: float32 [512, 512], P('feat')
- g_wproc2: float32 [512, 512], P('feat')
Inputs may be any that keep to these rules, and one draw needn't show every extreme that they name: `enc_send`: row j * 8 + r lists, for sender device j, the local grid rows of its slots to partition r in the first n slots and -1 after them; enc_dst's row of the receiver (r, f) for that sender partition has the same n live slots. A quarter of the partitions get half or more of the slots from every sender, and one gets all 2 from every sender. `enc_dst`: row (r * 4 + f) * 8 + s gives the target node, within partition r, of each slot that device s * 4 + f sends to device (r, f); -1 exactly where enc_send's slot is -1. `hal_send`: row s * 8 + r lists the rows of partition s sent to partition r; each pair has 1 to 4 live slots first, -1 after them; some pairs are full. `proc_src`: A value under 160 is a node of the edge's own partition; a value 160 + s * 4 + c names halo slot c from partition s, always a live one.
All inputs are finite; a program needn't handle non-finite values.
Results may differ from a plain program's by a relative error of at most 0.014.
Values may be sent and summed in bfloat16 or wider, within the bound.
A program may use at most 64 MiB of HBM per device.

v0:
```python
import math

import jax
import jax.numpy as jnp
from jax import lax
from jax.sharding import PartitionSpec as P

EPS = 1e-05


def matmul(left, right):
    return jnp.dot(left, right, preferred_element_type=jnp.float32)


def matmul_t(left, right):
    return lax.dot_general(
        left, right, (((left.ndim - 1,), (1,)), ((), ())), preferred_element_type=jnp.float32
    )


def outer(left, right):
    return lax.dot_general(
        left, right, (((0,), (0,)), ((), ())), preferred_element_type=jnp.float32
    )


def layer_norm(values):
    center = values - jnp.mean(values, axis=-1, keepdims=True)
    spread = jnp.mean(center * center, axis=-1, keepdims=True)
    scaling = lax.rsqrt(spread + EPS)
    return (center * scaling, scaling)


def norm_back(normed, scaling, upstream):
    inner = jnp.mean(upstream, axis=-1, keepdims=True)
    along = jnp.mean(upstream * normed, axis=-1, keepdims=True)
    return scaling * (upstream - inner - normed * along)


def silu_slope(preact):
    sigma = jax.nn.sigmoid(preact)
    return sigma * (1.0 + preact * (1.0 - sigma))


def edge_forward(preact, weight):
    hidden = jax.nn.silu(preact).astype(jnp.bfloat16)
    normed, scaling = layer_norm(matmul(hidden, weight))
    return (hidden, normed, scaling)


def pick_rows(source, indices):
    chosen = source[jnp.maximum(indices, 0)]
    return jnp.where((indices >= 0)[..., None], chosen, jnp.zeros((), source.dtype))


def per_device(
    grid_feat,
    mesh_feat,
    w_grid,
    w_mesh,
    w_enc2,
    w_src,
    w_dst,
    w_proc2,
    enc_send,
    enc_dst,
    hal_send,
    proc_src,
    proc_dst,
    cotangent,
):
    dom_count = lax.axis_size("dom")
    feat_count = lax.axis_size("feat")
    own_rows = mesh_feat.shape[0]
    latent_width = grid_feat.shape[1]
    part_rows = own_rows * feat_count
    slot_count = enc_send.shape[1]
    halo_count = hal_send.shape[1]
    factor = 1.0 / math.sqrt(own_rows * dom_count * feat_count)
    gathered = (
        lax.all_gather(w_grid, "feat", axis=0, tiled=True),
        lax.all_gather(w_mesh, "feat", axis=0, tiled=True),
        lax.all_gather(w_enc2, "feat", axis=0, tiled=True),
        lax.all_gather(w_src, "feat", axis=0, tiled=True),
        lax.all_gather(w_dst, "feat", axis=0, tiled=True),
        lax.all_gather(w_proc2, "feat", axis=0, tiled=True),
        lax.all_gather(mesh_feat, "feat", axis=0, tiled=True),
        lax.all_gather(cotangent, "feat", axis=0, tiled=True),
    )
    full_grid, full_mesh, full_enc2, full_src, full_dst, full_proc2, mesh_part, cot_part = gathered
    own_start = lax.axis_index("feat") * own_rows
    projected = matmul(grid_feat, full_grid).astype(jnp.bfloat16)
    outgoing = pick_rows(projected, enc_send)
    received = lax.all_to_all(outgoing, "dom", split_axis=0, concat_axis=0, tiled=True)
    node_proj = matmul(mesh_part, full_mesh)
    targets = jnp.maximum(enc_dst, 0).reshape(-1)
    valid = (enc_dst >= 0).reshape(-1, 1).astype(jnp.float32)
    preact = received.reshape(-1, latent_width).astype(jnp.float32) + node_proj[targets]
    hidden, normed, scaling = edge_forward(preact, full_enc2)
    partial_value = jax.ops.segment_sum(normed * valid, targets, num_segments=part_rows)
    summed = lax.psum(partial_value, "feat")
    latent = (mesh_part.astype(jnp.float32) + summed).astype(jnp.bfloat16)
    halo_rows = lax.all_to_all(
        pick_rows(latent, hal_send), "dom", split_axis=0, concat_axis=0, tiled=True
    )
    lookup = jnp.concatenate([latent, halo_rows.reshape(-1, latent_width)], axis=0)
    src_rows = lookup[proc_src]
    dst_rows = latent[proc_dst]
    preact_p = matmul(src_rows, full_src) + matmul(dst_rows, full_dst)
    hidden_p, normed_p, scaling_p = edge_forward(preact_p, full_proc2)
    partial_p = jax.ops.segment_sum(normed_p, proc_dst, num_segments=part_rows)
    summed_p = lax.psum(partial_p, "feat")
    result = (latent.astype(jnp.float32) + summed_p).astype(jnp.bfloat16)
    out_rows = lax.dynamic_slice_in_dim(result, own_start, own_rows, 0)
    cot_rows = cot_part.astype(jnp.float32)
    grad_mid_p = norm_back(normed_p, scaling_p, cot_rows[proc_dst]).astype(jnp.bfloat16)
    grad_pre_p = (matmul_t(grad_mid_p, full_proc2) * silu_slope(preact_p)).astype(jnp.bfloat16)
    g_lookup = jax.ops.segment_sum(
        matmul_t(grad_pre_p, full_src), proc_src, num_segments=lookup.shape[0]
    )
    g_local = g_lookup[:part_rows] + jax.ops.segment_sum(
        matmul_t(grad_pre_p, full_dst), proc_dst, num_segments=part_rows
    )
    halo_back = g_lookup[part_rows:].reshape(dom_count, halo_count, latent_width)
    returned = lax.all_to_all(halo_back, "dom", split_axis=0, concat_axis=0, tiled=True)
    returned = jnp.where((hal_send >= 0)[..., None], returned, jnp.zeros((), jnp.float32))
    g_local = g_local + jax.ops.segment_sum(
        returned.reshape(-1, latent_width),
        jnp.maximum(hal_send, 0).reshape(-1),
        num_segments=part_rows,
    )
    node_grad = lax.psum(g_local, "feat") + cot_rows
    grad_mid_e = norm_back(normed, scaling, node_grad[targets] * valid).astype(jnp.bfloat16)
    grad_pre_e = (matmul_t(grad_mid_e, full_enc2) * silu_slope(preact)).astype(jnp.bfloat16)
    mesh_back = jax.ops.segment_sum(
        matmul_t(grad_pre_e, full_mesh), targets, num_segments=part_rows
    )
    mesh_share = lax.psum_scatter(mesh_back, "feat", scatter_dimension=0, tiled=True)
    own_grad = lax.dynamic_slice_in_dim(node_grad, own_start, own_rows, 0)
    g_mesh = (own_grad + mesh_share).astype(jnp.bfloat16)
    slot_back = lax.all_to_all(
        grad_pre_e.reshape(dom_count, slot_count, latent_width),
        "dom",
        split_axis=0,
        concat_axis=0,
        tiled=True,
    )
    send_rows = jnp.maximum(enc_send, 0).reshape(-1)
    send_live = (enc_send >= 0).reshape(-1, 1).astype(jnp.float32)
    flat_back = slot_back.reshape(-1, latent_width)
    grid_back = matmul_t(flat_back, full_grid) * send_live
    g_grid = jax.ops.segment_sum(grid_back, send_rows, num_segments=grid_feat.shape[0]).astype(
        jnp.bfloat16
    )
    terms = (
        outer(grid_feat[send_rows], flat_back),
        outer(mesh_part[targets], grad_pre_e),
        outer(hidden, grad_mid_e),
        outer(src_rows, grad_pre_p),
        outer(dst_rows, grad_pre_p),
        outer(hidden_p, grad_mid_p),
    )
    shares = (
        lax.psum_scatter(
            terms[0].astype(jnp.bfloat16), "feat", scatter_dimension=0, tiled=True
        ).astype(jnp.float32),
        lax.psum_scatter(
            terms[1].astype(jnp.bfloat16), "feat", scatter_dimension=0, tiled=True
        ).astype(jnp.float32),
        lax.psum_scatter(
            terms[2].astype(jnp.bfloat16), "feat", scatter_dimension=0, tiled=True
        ).astype(jnp.float32),
        lax.psum_scatter(
            terms[3].astype(jnp.bfloat16), "feat", scatter_dimension=0, tiled=True
        ).astype(jnp.float32),
        lax.psum_scatter(
            terms[4].astype(jnp.bfloat16), "feat", scatter_dimension=0, tiled=True
        ).astype(jnp.float32),
        lax.psum_scatter(
            terms[5].astype(jnp.bfloat16), "feat", scatter_dimension=0, tiled=True
        ).astype(jnp.float32),
    )
    totals = lax.psum((shares[0], shares[1], shares[2], shares[3], shares[4], shares[5]), "dom")
    return (
        out_rows,
        g_grid,
        g_mesh,
        factor * totals[0],
        factor * totals[1],
        factor * totals[2],
        factor * totals[3],
        factor * totals[4],
        factor * totals[5],
    )


def solution(mesh):
    return jax.shard_map(
        per_device,
        mesh=mesh,
        in_specs=(
            P(("dom", "feat"), None),
            P(("dom", "feat"), None),
            P("feat", None),
            P("feat", None),
            P("feat", None),
            P("feat", None),
            P("feat", None),
            P("feat", None),
            P(("dom", "feat"), None),
            P(("dom", "feat"), None),
            P("dom", None),
            P(("dom", "feat")),
            P(("dom", "feat")),
            P(("dom", "feat"), None),
        ),
        out_specs=(
            P(("dom", "feat"), None),
            P(("dom", "feat"), None),
            P(("dom", "feat"), None),
            P("feat", None),
            P("feat", None),
            P("feat", None),
            P("feat", None),
            P("feat", None),
            P("feat", None),
        ),
        check_vma=False,
    )
```

profile of v0, /device:TPU:0, one launch (start us, length us, event | category | flops | bytes accessed | tf_op | source)
XLA Modules:
  0.0 440.8 jit_solution(10778965146168559237)
XLA Ops:
  9.8 8.9 %all_gather.25 = bf16[512,512]{1,0:T(8,128)(2,1)S(1)} all-gather(bf16[128,512]{1,0:T(8,128)(2,1)} %param.16), channel_id=1, replica_groups=mesh['dom'=8,'feat'=4] {'feat'}, dimensions={0}, use_global_device_ids=true | all-gather | bytes 655360 | tf_op jit(solution)/shard_map/all_gather | solution.py:81
  20.5 5.9 %all-to-all-start = ((bf16[8,2,512]{2,1,0:T(2,128)(2,1)}), bf16[8,2,512]{2,1,0:T(2,128)(2,1)S(1)}, u32[]{:S(2)}, u32[]{:S(2)}) async-start(bf16[8,2,512]{2,1,0:T(2,128)(2,1)} %broadcast_select_fusion.2), calls=%async_computation | async-start | bytes 32768 | tf_op jit(solution)/shard_map/all_to_all | solution.py:94
  27.9 5.5 %all_gather.24 = bf16[160,512]{1,0:T(8,128)(2,1)S(1)} all-gather(bf16[40,512]{1,0:T(8,128)(2,1)S(1)} %copy-done.25), channel_id=1, replica_groups=mesh['dom'=8,'feat'=4] {'feat'}, dimensions={0}, use_global_device_ids=true | all-gather | bytes 204800 | tf_op jit(solution)/shard_map/all_gather | solution.py:87
  33.4 7.4 %all_gather.26 = bf16[512,512]{1,0:T(8,128)(2,1)S(1)} all-gather(bf16[128,512]{1,0:T(8,128)(2,1)S(1)} %copy-done.17), channel_id=1, replica_groups=mesh['dom'=8,'feat'=4] {'feat'}, dimensions={0}, use_global_device_ids=true | all-gather | bytes 655360 | tf_op jit(solution)/shard_map/all_gather | solution.py:82
  40.8 7.8 %all_gather.27 = bf16[512,512]{1,0:T(8,128)(2,1)} all-gather(bf16[128,512]{1,0:T(8,128)(2,1)S(1)} %copy-done.18), channel_id=1, replica_groups=mesh['dom'=8,'feat'=4] {'feat'}, dimensions={0}, use_global_device_ids=true | all-gather | bytes 655360 | tf_op jit(solution)/shard_map/all_gather | solution.py:83
  48.6 7.4 %all_gather.28 = bf16[512,512]{1,0:T(8,128)(2,1)S(1)} all-gather(bf16[128,512]{1,0:T(8,128)(2,1)S(1)} %copy-done.19), channel_id=1, replica_groups=mesh['dom'=8,'feat'=4] {'feat'}, dimensions={0}, use_global_device_ids=true | all-gather | bytes 655360 | tf_op jit(solution)/shard_map/all_gather | solution.py:84
  56.0 7.3 %all_gather.29 = bf16[512,512]{1,0:T(8,128)(2,1)S(1)} all-gather(bf16[128,512]{1,0:T(8,128)(2,1)S(1)} %copy-done.20), channel_id=1, replica_groups=mesh['dom'=8,'feat'=4] {'feat'}, dimensions={0}, use_global_device_ids=true | all-gather | bytes 655360 | tf_op jit(solution)/shard_map/all_gather | solution.py:85
  64.3 5.5 %all_gather.31 = bf16[160,512]{1,0:T(8,128)(2,1)S(1)} all-gather(bf16[40,512]{1,0:T(8,128)(2,1)S(1)} %copy-done.26), channel_id=1, replica_groups=mesh['dom'=8,'feat'=4] {'feat'}, dimensions={0}, use_global_device_ids=true | all-gather | bytes 204800 | tf_op jit(solution)/shard_map/all_gather | solution.py:88
  72.1 1.6 gather_fusion.1
  76.2 1.6 scatter_custom_fusion
  78.7 7.8 %all_gather.30 = bf16[512,512]{1,0:T(8,128)(2,1)} all-gather(bf16[128,512]{1,0:T(8,128)(2,1)S(1)} %copy-done.21), channel_id=1, replica_groups=mesh['dom'=8,'feat'=4] {'feat'}, dimensions={0}, use_global_device_ids=true | all-gather | bytes 655360 | tf_op jit(solution)/shard_map/all_gather | solution.py:86
  86.5 25.0 %all-reduce.6.cloned.1.call-done = f32[160,512]{1,0:T(8,128)} async-done(((f32[160,512]{1,0:T(8,128)}), f32[160,512]{1,0:T(8,128)}) %all-reduce.6.cloned.1.call-update) | async-done | bytes 327696 | tf_op jit(solution)/shard_map/psum | solution.py:101
  114.5 5.6 %all-to-all-start.1 = ((bf16[8,4,512]{2,1,0:T(4,128)(2,1)}), bf16[8,4,512]{2,1,0:T(4,128)(2,1)S(1)}, u32[]{:S(2)}, u32[]{:S(2)}) async-start(bf16[8,4,512]{2,1,0:T(4,128)(2,1)} %broadcast_select_fusion.1), calls=%async_computation.1 | async-start | bytes 65536 | tf_op jit(solution)/shard_map/all_to_all | solution.py:103
  120.7 1.6 gather_fusion.4
  122.3 4.5 %all-to-all-done.1 = bf16[8,4,512]{2,1,0:T(4,128)(2,1)S(1)} async-done(((bf16[8,4,512]{2,1,0:T(4,128)(2,1)}), bf16[8,4,512]{2,1,0:T(4,128)(2,1)S(1)}, u32[]{:S(2)}, u32[]{:S(2)}) %all-to-all-start.1) | async-done | bytes 32800 | tf_op jit(solution)/shard_map/all_to_all | solution.py:103
  132.7 2.1 scatter_custom_fusion.2
  135.4 3.4 all-to-all-start.2
  139.9 2.3 scatter_custom_fusion.1
  143.2 1.7 scatter_fusion
  153.9 27.6 %all-reduce.8.cloned.1.call-done = (f32[160,512]{1,0:T(8,128)}, f32[160,512]{1,0:T(8,128)}) async-done(((f32[160,512]{1,0:T(8,128)}, f32[160,512]{1,0:T(8,128)}), (f32[160,512]{1,0:T(8,128)}, f32[160,512]{1,0:T(8,128)})) %all-reduce.8.cloned.1.call-update) | async-done | bytes 655376 | tf_op jit(solution)/shard_map/psum | solution.py:112
  184.5 1.5 scatter_custom_fusion.6
  191.6 5.5 %all-to-all-start.3 = ((bf16[8,2,512]{2,1,0:T(2,128)(2,1)}), bf16[8,2,512]{2,1,0:T(2,128)(2,1)S(1)}, u32[]{:S(2)}, u32[]{:S(2)}) async-start(bf16[8,2,512]{2,1,0:T(2,128)(2,1)} %reshape.159), calls=%async_computation.3 | async-start | bytes 32768 | tf_op jit(solution)/shard_map/all_to_all | solution.py:141
  197.8 5.9 %all-to-all-done.3 = bf16[8,2,512]{2,1,0:T(2,128)(2,1)S(1)} async-done(((bf16[8,2,512]{2,1,0:T(2,128)(2,1)}), bf16[8,2,512]{2,1,0:T(2,128)(2,1)S(1)}, u32[]{:S(2)}, u32[]{:S(2)}) %all-to-all-start.3) | async-done | bytes 16416 | tf_op jit(solution)/shard_map/all_to_all | solution.py:141
  205.7 1.5 fusion.16
  209.4 20.3 %reduce-scatter.18.cloned.1.call-done = bf16[128,512]{1,0:T(8,128)(2,1)} async-done(((bf16[512,512]{1,0:T(8,128)(2,1)}), bf16[128,512]{1,0:T(8,128)(2,1)}) %reduce-scatter.18.cloned.1.call-update) | async-done | bytes 131088 | tf_op jit(solution)/shard_map/reduce_scatter | solution.py:176
  229.7 24.0 %reduce-scatter.16.cloned.1.call-done = bf16[128,512]{1,0:T(8,128)(2,1)} async-done(((bf16[512,512]{1,0:T(8,128)(2,1)}), bf16[128,512]{1,0:T(8,128)(2,1)}) %reduce-scatter.16.cloned.1.call-update) | async-done | bytes 131088 | tf_op jit(solution)/shard_map/reduce_scatter | solution.py:173
  253.8 22.8 %reduce-scatter.8.cloned.1.call-done = f32[40,512]{1,0:T(8,128)} async-done(((f32[160,512]{1,0:T(8,128)}), f32[40,512]{1,0:T(8,128)}) %reduce-scatter.8.cloned.1.call-update) | async-done | bytes 81936 | tf_op jit(solution)/shard_map/reduce_scatter | solution.py:138
  276.5 1.5 add_convert_fusion.1
  278.1 22.7 %reduce-scatter.14.cloned.1.call-done = bf16[128,512]{1,0:T(8,128)(2,1)} async-done(((bf16[512,512]{1,0:T(8,128)(2,1)}), bf16[128,512]{1,0:T(8,128)(2,1)}) %reduce-scatter.14.cloned.1.call-update) | async-done | bytes 131088 | tf_op jit(solution)/shard_map/reduce_scatter | solution.py:170
  300.7 24.2 %reduce-scatter.12.cloned.1.call-done = bf16[128,512]{1,0:T(8,128)(2,1)} async-done(((bf16[512,512]{1,0:T(8,128)(2,1)}), bf16[128,512]{1,0:T(8,128)(2,1)}) %reduce-scatter.12.cloned.1.call-update) | async-done | bytes 131088 | tf_op jit(solution)/shard_map/reduce_scatter | solution.py:167
  324.9 24.2 %reduce-scatter.10.cloned.1.call-done = bf16[128,512]{1,0:T(8,128)(2,1)} async-done(((bf16[512,512]{1,0:T(8,128)(2,1)}), bf16[128,512]{1,0:T(8,128)(2,1)}) %reduce-scatter.10.cloned.1.call-update) | async-done | bytes 131088 | tf_op jit(solution)/shard_map/reduce_scatter | solution.py:164
  349.1 80.8 %all-reduce.9 = (f32[128,512]{1,0:T(8,128)S(1)}, f32[128,512]{1,0:T(8,128)S(1)}, f32[128,512]{1,0:T(8,128)S(1)}, f32[128,512]{1,0:T(8,128)S(1)}, f32[128,512]{1,0:T(8,128)S(1)}, /*index=5*/f32[128,512]{1,0:T(8,128)S(1)}) all-reduce(bf16[128,512]{1,0:T(8,128)(2,1)} %reduce-scatter.10.cloned.1.call-done,, ...), channel_id=1, replica_groups=mesh['dom'=8,'feat'=4] {'dom'}, use_global_device_ids=true, to_apply=%region_20.21 | all-reduce | flops 393216 | bytes 2359296 | tf_op jit(solution)/shard_map/psum | solution.py:183
  (211 shorter events, 51.1 us)
Async XLA Ops:
  7.2 11.5 %copy-start = (bf16[512,512]{1,0:T(8,128)(2,1)S(1)}, bf16[512,512]{1,0:T(8,128)(2,1)}, u32[]{:S(2)}) copy-start(bf16[512,512]{1,0:T(8,128)(2,1)} %param.14) | copy-start | bytes 1572868
  19.8 6.7 %copy-start.29 = (s32[8,4]{0,1:T(4,128)S(1)}, s32[8,4]{0,1:T(4,128)}, u32[]{:S(2)}) copy-start(s32[8,4]{0,1:T(4,128)} %param.24) | copy-start | bytes 388
  19.8 6.7 %copy-start.47 = (s32[160]{0:T(256)S(1)}, s32[160]{0:T(256)}, u32[]{:S(2)}) copy-start(s32[160]{0:T(256)} %param.25) | copy-start | bytes 1924
  19.8 7.3 %copy-start.39 = (s32[160]{0:T(256)S(1)}, s32[160]{0:T(256)}, u32[]{:S(2)}) copy-start(s32[160]{0:T(256)} %param.26) | copy-start | bytes 1924
  20.5 7.4 %copy-start.25 = (bf16[40,512]{1,0:T(8,128)(2,1)S(1)}, bf16[40,512]{1,0:T(8,128)(2,1)}, u32[]{:S(2)}) copy-start(bf16[40,512]{1,0:T(8,128)(2,1)} %param.15) | copy-start | bytes 122884
  20.5 53.2 %all-to-all-start = ((bf16[8,2,512]{2,1,0:T(2,128)(2,1)}), bf16[8,2,512]{2,1,0:T(2,128)(2,1)S(1)}, u32[]{:S(2)}, u32[]{:S(2)}) async-start(bf16[8,2,512]{2,1,0:T(2,128)(2,1)} %broadcast_select_fusion.2), calls=%async_computation | async-start | bytes 32768 | tf_op jit(solution)/shard_map/all_to_all | solution.py:94
  26.4 7.0 %copy-start.17 = (bf16[128,512]{1,0:T(8,128)(2,1)S(1)}, bf16[128,512]{1,0:T(8,128)(2,1)}, u32[]{:S(2)}) copy-start(bf16[128,512]{1,0:T(8,128)(2,1)} %param.17) | copy-start | bytes 393220
  26.4 85.0 %all-reduce.6.cloned.1.call-start = ((), (), s32[]{:S(2)}) async-start(), calls=%async_computation.11 | async-start | bytes 655360 | tf_op jit(solution)/shard_map/psum | solution.py:101
  27.9 44.2 %copy-start.34 = (s32[1024]{0:T(1024)}, s32[1024]{0:T(1024)S(1)}, u32[]{:S(2)}) copy-start(s32[1024]{0:T(1024)S(1)} %pad_clamp_fusion.4) | copy-start | bytes 12292
  33.4 29.9 %copy-start.1 = (bf16[160,512]{1,0:T(8,128)(2,1)}, bf16[160,512]{1,0:T(8,128)(2,1)S(1)}, u32[]{:S(2)}) copy-start(bf16[160,512]{1,0:T(8,128)(2,1)S(1)} %all_gather.24) | copy-start | bytes 491524
  33.4 7.4 %copy-start.18 = (bf16[128,512]{1,0:T(8,128)(2,1)S(1)}, bf16[128,512]{1,0:T(8,128)(2,1)}, u32[]{:S(2)}) copy-start(bf16[128,512]{1,0:T(8,128)(2,1)} %param.18) | copy-start | bytes 393220
  40.8 7.8 %copy-start.19 = (bf16[128,512]{1,0:T(8,128)(2,1)S(1)}, bf16[128,512]{1,0:T(8,128)(2,1)}, u32[]{:S(2)}) copy-start(bf16[128,512]{1,0:T(8,128)(2,1)} %param.19) | copy-start | bytes 393220
  48.6 7.4 %copy-start.20 = (bf16[128,512]{1,0:T(8,128)(2,1)S(1)}, bf16[128,512]{1,0:T(8,128)(2,1)}, u32[]{:S(2)}) copy-start(bf16[128,512]{1,0:T(8,128)(2,1)} %param.20) | copy-start | bytes 393220
  71.2 4.7 %copy-start.32 = (f32[16]{0:T(128)}, f32[16]{0:T(128)S(1)}, u32[]{:S(2)}) copy-start(f32[16]{0:T(128)S(1)} %reshape.162) | copy-start | bytes 196
  76.2 1.6 copy-start.35
  78.7 32.8 %copy-start.2 = (bf16[160,512]{1,0:T(8,128)(2,1)S(1)}, bf16[160,512]{1,0:T(8,128)(2,1)}, u32[]{:S(2)}) copy-start(bf16[160,512]{1,0:T(8,128)(2,1)} %copy-done.1) | copy-start | bytes 491524
  114.5 5.6 %copy-start.41 = (s32[160]{0:T(256)S(1)}, s32[160]{0:T(256)}, u32[]{:S(2)}) copy-start(s32[160]{0:T(256)} %compare_select_fusion.1) | copy-start | bytes 1924
  114.5 12.3 %all-to-all-start.1 = ((bf16[8,4,512]{2,1,0:T(4,128)(2,1)}), bf16[8,4,512]{2,1,0:T(4,128)(2,1)S(1)}, u32[]{:S(2)}, u32[]{:S(2)}) async-start(bf16[8,4,512]{2,1,0:T(4,128)(2,1)} %broadcast_select_fusion.1), calls=%async_computation.1 | async-start | bytes 65536 | tf_op jit(solution)/shard_map/all_to_all | solution.py:103
  135.4 10.2 %all-to-all-start.2 = ((f32[8,4,512]{2,1,0:T(4,128)}), f32[8,4,512]{2,1,0:T(4,128)S(1)}, u32[]{:S(2)}, u32[]{:S(2)}) async-start(f32[8,4,512]{2,1,0:T(4,128)} %reshape.157), calls=%async_computation.2 | async-start | bytes 131072 | tf_op jit(solution)/shard_map/all_to_all | solution.py:125
  138.8 42.7 %all-reduce.8.cloned.1.call-start = ((), (), s32[]{:S(2)}) async-start(), calls=%async_computation.19 | async-start | bytes 1310720 | tf_op jit(solution)/shard_map/psum | solution.py:112
  143.2 2.4 copy-start.38
  147.5 61.9 %reduce-scatter.20.cloned.1.call-start = ((), (), s32[]{:S(2)}) async-start(), calls=%async_computation.18 | async-start | bytes 655360 | tf_op jit(solution)/shard_map/reduce_scatter | solution.py:179
  149.7 80.1 %reduce-scatter.18.cloned.1.call-start = ((), (), s32[]{:S(2)}) async-start(), calls=%async_computation.17 | async-start | bytes 655360 | tf_op jit(solution)/shard_map/reduce_scatter | solution.py:176
  151.8 102.0 %reduce-scatter.16.cloned.1.call-start = ((), (), s32[]{:S(2)}) async-start(), calls=%async_computation.16 | async-start | bytes 655360 | tf_op jit(solution)/shard_map/reduce_scatter | solution.py:173
  153.8 27.6 %copy-start.8 = (bf16[160,512]{1,0:T(8,128)(2,1)S(1)}, bf16[160,512]{1,0:T(8,128)(2,1)}, u32[]{:S(2)}) copy-start(bf16[160,512]{1,0:T(8,128)(2,1)} %copy-done.7) | copy-start | bytes 491524
  153.8 122.7 %reduce-scatter.8.cloned.1.call-start = ((), (), s32[]{:S(2)}) async-start(), calls=%async_computation.12 | async-start | bytes 409600 | tf_op jit(solution)/shard_map/reduce_scatter | solution.py:138
  181.4 2.1 copy-start.4
  186.1 114.6 %reduce-scatter.14.cloned.1.call-start = ((), (), s32[]{:S(2)}) async-start(), calls=%async_computation.15 | async-start | bytes 655360 | tf_op jit(solution)/shard_map/reduce_scatter | solution.py:170
  187.5 137.4 %reduce-scatter.12.cloned.1.call-start = ((), (), s32[]{:S(2)}) async-start(), calls=%async_computation.14 | async-start | bytes 655360 | tf_op jit(solution)/shard_map/reduce_scatter | solution.py:167
  191.6 12.1 %all-to-all-start.3 = ((bf16[8,2,512]{2,1,0:T(2,128)(2,1)}), bf16[8,2,512]{2,1,0:T(2,128)(2,1)S(1)}, u32[]{:S(2)}, u32[]{:S(2)}) async-start(bf16[8,2,512]{2,1,0:T(2,128)(2,1)} %reshape.159), calls=%async_computation.3 | async-start | bytes 32768 | tf_op jit(solution)/shard_map/all_to_all | solution.py:141
  197.1 152.0 %reduce-scatter.10.cloned.1.call-start = ((), (), s32[]{:S(2)}) async-start(), calls=%async_computation.13 | async-start | bytes 655360 | tf_op jit(solution)/shard_map/reduce_scatter | solution.py:164
  209.4 139.7 %copy-start.24 = (bf16[128,512]{1,0:T(8,128)(2,1)S(1)}, bf16[128,512]{1,0:T(8,128)(2,1)}, u32[]{:S(2)}) copy-start(bf16[128,512]{1,0:T(8,128)(2,1)} %reduce-scatter.20.cloned.1.call-done) | copy-start | bytes 393220
  (29 other events, 23.9 us)
Sparse Core Ops, SparseCore 0:
  77.9 33.5 all-reduce.5
  147.6 33.7 all-reduce.7
  183.9 21.6 reduce-scatter.19
  208.0 21.7 reduce-scatter.17
  232.1 21.6 reduce-scatter.15
  256.1 20.3 reduce-scatter.7
  279.0 21.6 reduce-scatter.13
  303.2 21.6 reduce-scatter.11
  327.4 21.6 reduce-scatter.9
where the time goes:
time: 442 us; the launch traced here: 441 us
  waiting for transfers between devices  202 us (46%)
  blocking collectives  138 us (31%)
  other arithmetic  27.4 us (6%)
  local copies, waits for them, and re-layouts  23.9 us (5%)
  starting transfers between devices  21 us (5%)
  between operations  14.4 us (3%)
  matrix products  13.6 us (3%)
    psum x1, blocking collectives, per_device(): lax.psum((shares[0], shares[1], shares[2], shares[3], shares[4], shares[5...  80.8 us
    psum x1, waiting for transfers between devices, per_device(): summed_p = lax.psum(partial_p, 'feat')  27.6 us
    psum x1, waiting for transfers between devices, per_device(): summed = lax.psum(partial_value, 'feat')  25 us
    reduce_scatter x1, waiting for transfers between devices, per_device(): lax.psum_scatter(terms[0].astype(jnp.bfloat16), 'feat', scatter_dimension...  24.2 us
    reduce_scatter x1, waiting for transfers between devices, per_device(): lax.psum_scatter(terms[1].astype(jnp.bfloat16), 'feat', scatter_dimension...  24.2 us
    reduce_scatter x1, waiting for transfers between devices, per_device(): lax.psum_scatter(terms[3].astype(jnp.bfloat16), 'feat', scatter_dimension...  24 us
    reduce_scatter x1, waiting for transfers between devices, per_device(): lax.psum_scatter(mesh_back, 'feat', scatter_dimension=0, tiled=True)  22.8 us
    reduce_scatter x1, waiting for transfers between devices, per_device(): lax.psum_scatter(terms[2].astype(jnp.bfloat16), 'feat', scatter_dimension...  22.7 us
  transfers between devices with their start and end apart: 13, of which 11 were waited for; matrix products, arithmetic and copies ran while one was open for 7% of the time, Pallas kernels for 0%

commit v1 on v0

--- a/solution.py
+++ b/solution.py
@@ -1,11 +1,19 @@
+import functools
 import math
 
 import jax
 import jax.numpy as jnp
 from jax import lax
+from jax.experimental import pallas as pl
+from jax.experimental.pallas import tpu as pltpu
 from jax.sharding import PartitionSpec as P
 
 EPS = 1e-05
+BF16 = jnp.bfloat16
+F32 = jnp.float32
+MESH_ID = pl.DeviceIdType.MESH
+SLAB = 8
+TILE = 16
 
 
 def matmul(left, right):
@@ -194,9 +202,454 @@
     )
 
 
+def pick(hot, rows):
+    return matmul(hot, rows).astype(BF16)
+
+
+def halves(values):
+    high = values.astype(BF16)
+    return (high, (values - high.astype(F32)).astype(BF16))
+
+
+def pick_wide(hot, values):
+    high, low = halves(values)
+    return matmul(hot, high) + matmul(hot, low)
+
+
+def spread(hot, values):
+    high, low = halves(values)
+    return outer(hot, high) + outer(hot, low)
+
+
+def hot_rows(indices, width):
+    columns = lax.broadcasted_iota(jnp.int32, (indices.shape[0], width), 1)
+    return jnp.where(columns == indices, 1.0, 0.0).astype(BF16)
+
+
+def hidden_and_slope(preact):
+    sigma = 1.0 / (1.0 + jnp.exp(-preact))
+    return ((preact * sigma).astype(BF16), sigma * (1.0 + preact * (1.0 - sigma)))
+
+
+def fused_kernel(
+    sizes,
+    grid_ref,
+    mesh_ref,
+    wg_ref,
+    wm_ref,
+    we_ref,
+    ws_ref,
+    wd_ref,
+    wp_ref,
+    index_ref,
+    cot_ref,
+    out_ref,
+    ggrid_ref,
+    gmesh_ref,
+    o_wg,
+    o_wm,
+    o_we,
+    o_ws,
+    o_wd,
+    o_wp,
+    weights,
+    mesh_buf,
+    cot_buf,
+    slot_out,
+    slot_in,
+    halo_out,
+    halo_in,
+    halo_bout,
+    halo_bin,
+    slot_bout,
+    slot_bin,
+    sum_buf,
+    share_out,
+    share_in,
+    term,
+    pair_in,
+    cross_out,
+    cross_in,
+    ring_out,
+    ring_in,
+    total_buf,
+    gather_sems,
+    dom_sems,
+    sum_sems,
+    share_sems,
+    pair_sems,
+    cross_sems,
+):
+    dom, feat, own, part, edges = sizes
+    me = lax.axis_index("dom")
+    f = lax.axis_index("feat")
+    f1 = f + 1 - 2 * lax.rem(f, 2)
+    f2 = lax.rem(f + 2, feat)
+    f3 = lax.rem(f1 + 2, feat)
+    factor = 1.0 / math.sqrt(own * dom * feat)
+
+    def send(src, dst, sems, slot, **where):
+        copy = pltpu.make_async_remote_copy(
+            src_ref=src,
+            dst_ref=dst,
+            send_sem=sems.at[(0,) + slot],
+            recv_sem=sems.at[(1,) + slot],
+            device_id=where,
+            device_id_type=MESH_ID,
+        )
+        copy.start()
+        return copy
+
+    def finish(copies):
+        for copy in copies:
+            copy.wait()
+
+    def dom_exchange(kind, src, dst):
+        copies = []
+        for step in range(1, dom):
+            peer = lax.rem(me + step, dom)
+            copies.append(send(src.at[peer], dst.at[me], dom_sems, (kind, step), dom=peer))
+        dst[me] = src[me]
+        return copies
+
+    def put_slabs(ref, rows):
+        for index in range(dom):
+            ref[index] = rows[index * SLAB : (index + 1) * SLAB].astype(BF16)
+
+    def get_slabs(ref):
+        return jnp.concatenate([ref[index].astype(F32) for index in range(dom)], axis=0).astype(BF16)
+
+    def all_parts(ref):
+        return jnp.concatenate([ref[index].astype(F32) for index in range(feat)], axis=0)
+
+    barrier = pltpu.get_barrier_semaphore()
+    for step in range(1, dom):
+        pl.semaphore_signal(
+            barrier, inc=1, device_id={"dom": lax.rem(me + step, dom)}, device_id_type=MESH_ID
+        )
+    for step in range(1, feat):
+        pl.semaphore_signal(
+            barrier, inc=1, device_id={"feat": lax.rem(f + step, feat)}, device_id_type=MESH_ID
+        )
+    mesh_buf[f] = mesh_ref[...]
+    cot_buf[f] = cot_ref[...]
+    slots = dom * SLAB
+    send_hot = hot_rows(index_ref[0:slots], grid_ref.shape[0])
+    put_slabs(slot_out, matmul(send_hot, grid_ref[...]))
+    pl.semaphore_wait(barrier, dom + feat - 2)
+
+    slot_copies = dom_exchange(0, slot_out, slot_in)
+    pieces = [
+        (wg_ref, lambda g: weights.at[0, g]),
+        (mesh_buf.at[f], lambda g: mesh_buf.at[g]),
+        (wm_ref, lambda g: weights.at[1, g]),
+        (we_ref, lambda g: weights.at[2, g]),
+        (ws_ref, lambda g: weights.at[3, g]),
+        (wd_ref, lambda g: weights.at[4, g]),
+        (wp_ref, lambda g: weights.at[5, g]),
+        (cot_buf.at[f], lambda g: cot_buf.at[g]),
+    ]
+    across, beside, passed = [], [], []
+    for slot, (src, dst) in enumerate(pieces):
+        across.append(send(src, dst(f), gather_sems, (0, slot), feat=f2))
+        beside.append(send(src, dst(f), gather_sems, (1, slot), feat=f1))
+    for slot, src in enumerate((wg_ref, wm_ref, we_ref, ws_ref, wd_ref, wp_ref)):
+        weights[slot, f] = src[...]
+    for slot, (src, dst) in enumerate(pieces):
+        across[slot].wait_recv()
+        passed.append(send(dst(f2), dst(f2), gather_sems, (2, slot), feat=f1))
+
+    def whole(slot):
+        return weights[slot].reshape(feat * weights.shape[2], weights.shape[3])
+
+    def arrived(slot):
+        beside[slot].wait_recv()
+        passed[slot].wait_recv()
+
+    target_hot = hot_rows(index_ref[slots : 2 * slots], part)
+    finish(slot_copies)
+    grid_rows = get_slabs(slot_in)
+    for slot in (0, 1, 2, 3):
+        arrived(slot)
+    mesh_part = all_parts(mesh_buf)
+    mesh_rows = pick(target_hot, mesh_part.astype(BF16))
+    preact_e = pick(grid_rows, whole(0)).astype(F32) + matmul(mesh_rows, whole(1))
+    hidden_e, slope_e = hidden_and_slope(preact_e)
+    normed_e, scaling_e = layer_norm(matmul(hidden_e, whole(2)))
+
+    def feat_sum(kind, value):
+        first = value.astype(BF16)
+        sum_buf[kind, 0] = first
+        copy = send(sum_buf.at[kind, 0], sum_buf.at[kind, 1], sum_sems, (kind, 0), feat=f1)
+        yield
+        copy.wait()
+        both = (first.astype(F32) + sum_buf[kind, 1].astype(F32)).astype(BF16)
+        sum_buf[kind, 2] = both
+        copy = send(sum_buf.at[kind, 2], sum_buf.at[kind, 3], sum_sems, (kind, 1), feat=f2)
+        yield
+        copy.wait()
+        yield both.astype(F32) + sum_buf[kind, 3].astype(F32)
+
+    stages = feat_sum(0, spread(target_hot, normed_e))
+    next(stages)
+    next(stages)
+    halo_hot = hot_rows(index_ref[2 * slots : 3 * slots], part)
+    source_hot = hot_rows(index_ref[3 * slots : 3 * slots + edges], part + slots)
+    edge_hot = hot_rows(index_ref[3 * slots + edges : 3 * slots + 2 * edges], part)
+    latent = (mesh_part + next(stages)).astype(BF16)
+
+    put_slabs(halo_out, matmul(halo_hot, latent))
+    halo_copies = dom_exchange(1, halo_out, halo_in)
+    dst_rows = pick(edge_hot, latent)
+    for slot in (4, 5, 6, 7):
+        arrived(slot)
+    pre_dst = matmul(dst_rows, whole(4))
+    upstream_p = matmul(edge_hot, all_parts(cot_buf).astype(BF16))
+    finish(halo_copies)
+    lookup = jnp.concatenate([latent, get_slabs(halo_in)], axis=0)
+    src_rows = pick(source_hot, lookup)
+    preact_p = matmul(src_rows, whole(3)) + pre_dst
+    hidden_p, slope_p = hidden_and_slope(preact_p)
+    normed_p, scaling_p = layer_norm(matmul(hidden_p, whole(5)))
+
+    mid_p = norm_back(normed_p, scaling_p, upstream_p).astype(BF16)
+    grad_p = (matmul_t(mid_p, whole(5)) * slope_p).astype(BF16)
+    g_lookup = spread(source_hot, matmul_t(grad_p, whole(3)))
+    put_slabs(halo_bout, g_lookup[part:])
+    back_copies = dom_exchange(2, halo_bout, halo_bin)
+    g_local = g_lookup[:part] + spread(edge_hot, matmul_t(grad_p, whole(4)))
+
+    def scatter_own(kind, value):
+        for index in range(feat):
+            share_out[kind, index] = value[index * own : (index + 1) * own].astype(BF16)
+        copies = []
+        for step in range(1, feat):
+            peer = lax.rem(f + step, feat)
+            copies.append(
+                send(
+                    share_out.at[kind, peer],
+                    share_in.at[kind, f],
+                    share_sems,
+                    (kind, step),
+                    feat=peer,
+                )
+            )
+        share_in[kind, f] = share_out[kind, f]
+        return copies
+
+    def own_sum(kind):
+        total = share_in[kind, 0].astype(F32)
+        for index in range(1, feat):
+            total = total + share_in[kind, index].astype(F32)
+        return total
+
+    rows = term.shape[3]
+    chunk = ring_out.shape[3]
+
+    def start_terms(group, left, right):
+        for index in range(3):
+            product = outer(left[index], right[index]).astype(BF16)
+            for shard in range(feat):
+                term[group, shard, index] = product[shard * rows : (shard + 1) * rows]
+        return [
+            send(term.at[group, f1], pair_in.at[group, 0], pair_sems, (group, 0), feat=f1),
+            send(term.at[group, f3], pair_in.at[group, 1], pair_sems, (group, 1), feat=f1),
+        ]
+
+    def cross_terms(group, copies):
+        finish(copies)
+        for index in range(3):
+            cross_out[group, index] = (
+                term[group, f2, index].astype(F32) + pair_in[group, 1, index].astype(F32)
+            ).astype(BF16)
+        return [send(cross_out.at[group], cross_in.at[group], cross_sems, (group,), feat=f2)]
+
+    def ring_terms(group, copies):
+        finish(copies)
+        for index in range(3):
+            share = (
+                term[group, f, index].astype(F32)
+                + pair_in[group, 0, index].astype(F32)
+                + cross_in[group, index].astype(F32)
+            ).astype(BF16)
+            for piece in range(dom):
+                ring_out[group, piece, index] = share[piece * chunk : (piece + 1) * chunk]
+        return dom_exchange(4 + 2 * group, ring_out.at[group], ring_in.at[group])
+
+    def total_terms(group, copies):
+        finish(copies)
+        for index in range(3):
+            total = ring_in[group, 0, index].astype(F32)
+            for piece in range(1, dom):
+                total = total + ring_in[group, piece, index].astype(F32)
+            total_buf[group, me, index] = total.astype(BF16)
+        copies = []
+        for step in range(1, dom):
+            peer = lax.rem(me + step, dom)
+            copies.append(
+                send(
+                    total_buf.at[group, me],
+                    total_buf.at[group, me],
+                    dom_sems,
+                    (5 + 2 * group, step),
+                    dom=peer,
+                )
+            )
+        return copies
+
+    def write_terms(group, copies, refs):
+        finish(copies)
+        for index, ref in enumerate(refs):
+            for piece in range(dom):
+                ref[piece * chunk : (piece + 1) * chunk] = factor * total_buf[
+                    group, piece, index
+                ].astype(F32)
+
+    proc_pair = start_terms(0, (src_rows, dst_rows, hidden_p), (grad_p, grad_p, mid_p))
+    finish(back_copies)
+    g_local = g_local + outer(halo_hot, get_slabs(halo_bin))
+    stages = feat_sum(1, g_local)
+    next(stages)
+    next(stages)
+    proc_share = scatter_own(0, spread(edge_hot, normed_p))
+    proc_cross = cross_terms(0, proc_pair)
+    cot_part = all_parts(cot_buf)
+    node_grad = next(stages) + cot_part
+
+    mid_e = norm_back(normed_e, scaling_e, pick_wide(target_hot, node_grad)).astype(BF16)
+    grad_e = (matmul_t(mid_e, whole(2)) * slope_e).astype(BF16)
+    enc_pair = start_terms(1, (grid_rows, mesh_rows, hidden_e), (grad_e, grad_e, mid_e))
+    put_slabs(slot_bout, grad_e.astype(F32))
+    slot_copies = dom_exchange(3, slot_bout, slot_bin)
+    enc_share = scatter_own(1, spread(target_hot, matmul_t(grad_e, whole(1))))
+    enc_cross = cross_terms(1, enc_pair)
+    proc_ring = ring_terms(0, proc_cross)
+    own_hot = hot_rows(
+        f * own + lax.broadcasted_iota(jnp.int32, (own, 1), 0), part
+    )
+    own_grad = pick_wide(own_hot, node_grad)
+    own_latent = matmul(own_hot, latent)
+    finish(slot_copies)
+    slot_rows = outer(send_hot, get_slabs(slot_bin)).astype(BF16)
+    ggrid_ref[...] = matmul_t(slot_rows, whole(0)).astype(BF16)
+    finish(proc_share)
+    out_ref[...] = (own_latent + own_sum(0)).astype(BF16)
+    proc_total = total_terms(0, proc_ring)
+    enc_ring = ring_terms(1, enc_cross)
+    finish(enc_share)
+    gmesh_ref[...] = (own_grad + own_sum(1)).astype(BF16)
+    enc_total = total_terms(1, enc_ring)
+    write_terms(0, proc_total, (o_ws, o_wd, o_wp))
+    write_terms(1, enc_total, (o_wg, o_wm, o_we))
+    for copies in (across, beside, passed):
+        for copy in copies:
+            copy.wait_send()
+
+
+def fused(
+    grid_feat,
+    mesh_feat,
+    w_grid,
+    w_mesh,
+    w_enc2,
+    w_src,
+    w_dst,
+    w_proc2,
+    enc_send,
+    enc_dst,
+    hal_send,
+    proc_src,
+    proc_dst,
+    cotangent,
+):
+    dom = lax.axis_size("dom")
+    feat = lax.axis_size("feat")
+    own, width = mesh_feat.shape
+    part = own * feat
+    edges = proc_src.shape[0]
+    halo = hal_send.shape[1]
+    shard = w_grid.shape[0]
+    chunk = shard // dom
+
+    def slabs(table):
+        return jnp.pad(table, ((0, 0), (0, SLAB - table.shape[1])), constant_values=-1).reshape(-1)
+
+    far = proc_src - part
+    moved = jnp.where(far < 0, proc_src, part + far // halo * SLAB + far % halo)
+    indices = jnp.concatenate([slabs(enc_send), slabs(enc_dst), slabs(hal_send), moved, proc_dst])
+    slab = pltpu.VMEM((dom, SLAB, width), BF16)
+    vmem = pl.BlockSpec(memory_space=pltpu.VMEM)
+    weight_out = jax.ShapeDtypeStruct((shard, width), F32)
+    return pl.pallas_call(
+        functools.partial(fused_kernel, (dom, feat, own, part, edges)),
+        out_shape=(
+            jax.ShapeDtypeStruct((own, width), BF16),
+            jax.ShapeDtypeStruct(grid_feat.shape, BF16),
+            jax.ShapeDtypeStruct((own, width), BF16),
+        )
+        + (weight_out,) * 6,
+        in_specs=[vmem] * 10,
+        out_specs=(vmem,) * 9,
+        scratch_shapes=[
+            pltpu.VMEM((6, feat, shard, width), BF16),
+            pltpu.VMEM((feat, own, width), BF16),
+            pltpu.VMEM((feat, own, width), BF16),
+            slab,
+            slab,
+            slab,
+            slab,
+            slab,
+            slab,
+            slab,
+            slab,
+            pltpu.VMEM((2, 4, part, width), BF16),
+            pltpu.VMEM((2, feat, own, width), BF16),
+            pltpu.VMEM((2, feat, own, width), BF16),
+            pltpu.VMEM((2, feat, 3, shard, width), BF16),
+            pltpu.VMEM((2, 2, 3, shard, width), BF16),
+            pltpu.VMEM((2, 3, shard, width), BF16),
+            pltpu.VMEM((2, 3, shard, width), BF16),
+            pltpu.VMEM((2, dom, 3, chunk, width), BF16),
+            pltpu.VMEM((2, dom, 3, chunk, width), BF16),
+            pltpu.VMEM((2, dom, 3, chunk, width), BF16),
+            pltpu.SemaphoreType.DMA((2, 3, 8)),
+            pltpu.SemaphoreType.DMA((2, 8, dom)),
+            pltpu.SemaphoreType.DMA((2, 2, 2)),
+            pltpu.SemaphoreType.DMA((2, 2, feat)),
+            pltpu.SemaphoreType.DMA((2, 2, 2)),
+            pltpu.SemaphoreType.DMA((2, 2)),
+        ],
+        compiler_params=pltpu.CompilerParams(
+            collective_id=0, has_side_effects=True, vmem_limit_bytes=56 * 1024 * 1024
+        ),
+        name="fused_layer",
+    )(
+        grid_feat,
+        mesh_feat,
+        w_grid,
+        w_mesh,
+        w_enc2,
+        w_src,
+        w_dst,
+        w_proc2,
+        indices[:, None],
+        cotangent,
+    )
+
+
+def choose(*args):
+    dom = lax.axis_size("dom")
+    feat = lax.axis_size("feat")
+    shard = args[2].shape[0]
+    fits = max(args[8].shape[1], args[10].shape[1]) <= SLAB
+    if feat == 4 and shard % (dom * TILE) == 0 and fits:
+        return fused(*args)
+    return per_device(*args)
+
+
 def solution(mesh):
     return jax.shard_map(
-        per_device,
+        choose,
         mesh=mesh,
         in_specs=(
             P(("dom", "feat"), None),

time: 442 us -> 118 us (0.27)
  waiting for transfers between devices: 202 us -> 0 us
  blocking collectives: 138 us -> 0 us
  Pallas kernels: 0 us -> 103 us
  other arithmetic: 27.4 us -> 0.7 us
  starting transfers between devices: 21 us -> 0 us
  between operations: 14.4 us -> 0.69 us
  matrix products: 13.6 us -> 0 us
  local copies, waits for them, and re-layouts: 23.9 us -> 13.1 us
    reduce_scatter x7 -> x0, waiting for transfers between devices: 138 us -> none  [the longest x1 24.2 us: per_device(): lax.psum_scatter(terms[0].astype(jnp.bfloat16), 'feat', scatter_dimension...]
    pallas_call x0 -> x1, Pallas kernels: none -> 103 us  [fused(): pl.pallas_call(functools.partial(fused_kernel, (dom, feat, own, part, edg...]
    psum x1 -> x0, blocking collectives: 80.8 us -> none  [per_device(): lax.psum((shares[0], shares[1], shares[2], shares[3], shares[4], shares[5...]
    all_gather x8 -> x0, blocking collectives: 57.6 us -> none  [the longest x1 8.87 us: per_device(): lax.all_gather(w_grid, 'feat', axis=0, tiled=True)]
    psum x2 -> x0, waiting for transfers between devices: 52.5 us -> none  [the longest x1 27.6 us: per_device(): summed_p = lax.psum(partial_p, 'feat')]
    all_to_all x4 -> x0, starting transfers between devices: 20.4 us -> none  [the longest x1 5.94 us: per_device(): lax.all_to_all(outgoing, 'dom', split_axis=0, concat_axis=0, tiled=True)]
    dot_general x18 -> x0, matrix products: 13.6 us -> none  [the longest x6 6.88 us: outer(): lax.dot_general(left, right, (((0,), (0,)), ((), ())), preferred_element_...]
    scatter-add x7 -> x0, other arithmetic: 11.2 us -> none  [the longest x1 2.33 us: per_device(): partial_p = jax.ops.segment_sum(normed_p, proc_dst, num_segments=part_rows)]
  transfers between devices with their start and end apart: 13 -> 0, of which waited for: 11 -> 0; matrix products, arithmetic and copies ran while one was open for 7% -> 0% of each run, Pallas kernels for 0% -> 0%
where the time goes in v1:
time: 118 us
  Pallas kernels  103 us (87%)
  local copies, waits for them, and re-layouts  13.1 us (11%)
    pallas_call x1, Pallas kernels, fused(): pl.pallas_call(functools.partial(fused_kernel, (dom, feat, own, part, edg...  103 us
    unnamed x34, local copies, waits for them, and re-layouts  11.9 us

profile of v1, /device:TPU:0, one launch (start us, length us, event | category | flops | bytes accessed | tf_op | source)
XLA Modules:
  0.0 117.6 jit_solution(12987812672676717877)
XLA Ops:
  0.6 0.0 copy-start.8
  0.7 0.7 fusion.1
  1.4 0.0 copy-done.8
  1.4 0.1 copy.30
  1.4 0.0 copy-start.9
  1.5 0.1 reshape.27
  1.5 0.6 copy-done.9
  2.1 0.1 copy.31
  2.2 0.1 reshape.28
  2.3 0.6 copy-done.7
  2.9 0.1 copy.32
  3.0 0.1 reshape.29
  3.1 0.6 copy-done.10
  3.7 0.1 concatenate.3
  3.7 0.9 copy.29.index_ref
  4.6 103.1 %fused_layer.1 = (bf16[40,512]{1,0:T(8,128)(2,1)}, bf16[512,512]{1,0:T(8,128)(2,1)}, bf16[40,512]{1,0:T(8,128)(2,1)}, f32[128,512]{1,0:T(8,128)}, f32[128,512]{1...) custom-call(bf16[512,512]{1,0:T(8,128)(2,1)} %grid_ref.1, ...), custom_call_target="tpu_custom_call" | custom-call | tf_op jit(solution)/shard_map/fused_layer/pallas_call | solution.py:583
  107.7 1.4 %copy.42 = bf16[40,512]{1,0:T(8,128)(2,1)} copy(bf16[40,512]{1,0:T(8,128)(2,1)} %get-tuple-element.18) | data formatting | bytes 81920
  109.1 1.9 %copy.43 = bf16[512,512]{1,0:T(8,128)(2,1)} copy(bf16[512,512]{1,0:T(8,128)(2,1)} %get-tuple-element.19) | data formatting | bytes 1048576
  111.0 0.0 copy-done.6
  111.0 0.6 copy.44
  111.6 0.0 copy-done.5
  111.6 0.7 copy.45
  112.4 0.3 copy-done.4
  112.7 0.7 copy.46
  113.4 0.3 copy-done.3
  113.7 0.7 copy.47
  114.4 0.3 copy-done.2
  114.8 0.7 copy.48
  115.5 0.3 copy-done.1
  115.8 0.7 copy.49
  116.5 0.3 copy-done
  116.9 0.7 copy.50
  (12 shorter events, 0.0 us)
Async XLA Ops:
  0.6 0.7 copy-start.8
  1.4 0.7 copy-start.9
  2.2 0.7 copy-start.7
  3.0 0.7 copy-start.10
  109.1 1.9 %copy-start.6 = (bf16[40,512]{1,0:T(8,128)(2,1)S(1)}, bf16[40,512]{1,0:T(8,128)(2,1)}, u32[]{:S(2)}) copy-start(bf16[40,512]{1,0:T(8,128)(2,1)} %get-tuple-element.20) | copy-start | bytes 122884
  109.1 2.5 %copy-start.5 = (f32[128,512]{1,0:T(8,128)S(1)}, f32[128,512]{1,0:T(8,128)}, u32[]{:S(2)}) copy-start(f32[128,512]{1,0:T(8,128)} %get-tuple-element.21) | copy-start | bytes 786436
  111.6 1.0 copy-start.4
  112.7 1.0 copy-start.3
  113.7 1.0 copy-start.2
  114.8 1.0 copy-start.1
  115.8 1.0 copy-start

commit v2 on v1

--- a/solution.py
+++ b/solution.py
@@ -246,12 +246,7 @@
     out_ref,
     ggrid_ref,
     gmesh_ref,
-    o_wg,
-    o_wm,
-    o_we,
-    o_ws,
-    o_wd,
-    o_wp,
+    terms_ref,
     weights,
     mesh_buf,
     cot_buf,
@@ -286,7 +281,6 @@
     f1 = f + 1 - 2 * lax.rem(f, 2)
     f2 = lax.rem(f + 2, feat)
     f3 = lax.rem(f1 + 2, feat)
-    factor = 1.0 / math.sqrt(own * dom * feat)
 
     def send(src, dst, sems, slot, **where):
         copy = pltpu.make_async_remote_copy(
@@ -339,25 +333,55 @@
     pl.semaphore_wait(barrier, dom + feat - 2)
 
     slot_copies = dom_exchange(0, slot_out, slot_in)
-    pieces = [
-        (wg_ref, lambda g: weights.at[0, g]),
-        (mesh_buf.at[f], lambda g: mesh_buf.at[g]),
-        (wm_ref, lambda g: weights.at[1, g]),
-        (we_ref, lambda g: weights.at[2, g]),
-        (ws_ref, lambda g: weights.at[3, g]),
-        (wd_ref, lambda g: weights.at[4, g]),
-        (wp_ref, lambda g: weights.at[5, g]),
-        (cot_buf.at[f], lambda g: cot_buf.at[g]),
-    ]
-    across, beside, passed = [], [], []
-    for slot, (src, dst) in enumerate(pieces):
-        across.append(send(src, dst(f), gather_sems, (0, slot), feat=f2))
-        beside.append(send(src, dst(f), gather_sems, (1, slot), feat=f1))
-    for slot, src in enumerate((wg_ref, wm_ref, we_ref, ws_ref, wd_ref, wp_ref)):
+    refs = (wg_ref, wm_ref, we_ref, ws_ref, wd_ref, wp_ref)
+    half = wg_ref.shape[0] // 2
+    beyond = me + 1 - 2 * lax.rem(me, 2)
+    mine = pl.ds(pl.multiple_of(lax.rem(me, 2) * half, half), half)
+    theirs = pl.ds(pl.multiple_of((1 - lax.rem(me, 2)) * half, half), half)
+    across, beside, passed, sideways, closing = {}, {}, {}, {}, {}
+
+    def start_small(slot, buf):
+        across[slot] = send(buf.at[f], buf.at[f], gather_sems, (0, slot), feat=f2)
+        beside[slot] = send(buf.at[f], buf.at[f], gather_sems, (1, slot), feat=f1)
+
+    def start_weight(slot):
+        src, dst = refs[slot], weights.at[slot, f]
+        across[slot] = send(src.at[mine], dst.at[mine], gather_sems, (0, slot), feat=f2)
+        beside[slot] = send(src, dst, gather_sems, (1, slot), feat=f1)
+
+    def relay_small(slot, buf):
+        across[slot].wait_recv()
+        passed[slot] = send(buf.at[f2], buf.at[f2], gather_sems, (2, slot), feat=f1)
+
+    def relay(slot):
+        across[slot].wait_recv()
+        part_ref = weights.at[slot, f2, mine]
+        sideways[slot] = send(part_ref, part_ref, gather_sems, (3, slot), dom=beyond)
+        passed[slot] = send(part_ref, part_ref, gather_sems, (2, slot), feat=f1)
+
+    def close(slot):
+        sideways[slot].wait_recv()
+        part_ref = weights.at[slot, f2, theirs]
+        closing[slot] = send(part_ref, part_ref, gather_sems, (4, slot), feat=f1)
+
+    start_weight(0)
+    start_small(6, mesh_buf)
+    for slot in (1, 2, 3, 4, 5):
+        start_weight(slot)
+    start_small(7, cot_buf)
+    for slot, src in enumerate(refs):
         weights[slot, f] = src[...]
-    for slot, (src, dst) in enumerate(pieces):
-        across[slot].wait_recv()
-        passed.append(send(dst(f2), dst(f2), gather_sems, (2, slot), feat=f1))
+    relay(0)
+    relay_small(6, mesh_buf)
+    relay(1)
+    relay(2)
+    close(0)
+    relay(3)
+    close(1)
+    relay(4)
+    close(2)
+    relay(5)
+    relay_small(7, cot_buf)
 
     def whole(slot):
         return weights[slot].reshape(feat * weights.shape[2], weights.shape[3])
@@ -365,11 +389,13 @@
     def arrived(slot):
         beside[slot].wait_recv()
         passed[slot].wait_recv()
+        if slot in closing:
+            closing[slot].wait_recv()
 
     target_hot = hot_rows(index_ref[slots : 2 * slots], part)
     finish(slot_copies)
     grid_rows = get_slabs(slot_in)
-    for slot in (0, 1, 2, 3):
+    for slot in (0, 6, 1, 2):
         arrived(slot)
     mesh_part = all_parts(mesh_buf)
     mesh_rows = pick(target_hot, mesh_part.astype(BF16))
@@ -393,6 +419,8 @@
     stages = feat_sum(0, spread(target_hot, normed_e))
     next(stages)
     next(stages)
+    for slot in (3, 4, 5):
+        close(slot)
     halo_hot = hot_rows(index_ref[2 * slots : 3 * slots], part)
     source_hot = hot_rows(index_ref[3 * slots : 3 * slots + edges], part + slots)
     edge_hot = hot_rows(index_ref[3 * slots + edges : 3 * slots + 2 * edges], part)
@@ -401,7 +429,7 @@
     put_slabs(halo_out, matmul(halo_hot, latent))
     halo_copies = dom_exchange(1, halo_out, halo_in)
     dst_rows = pick(edge_hot, latent)
-    for slot in (4, 5, 6, 7):
+    for slot in (3, 4, 5, 7):
         arrived(slot)
     pre_dst = matmul(dst_rows, whole(4))
     upstream_p = matmul(edge_hot, all_parts(cot_buf).astype(BF16))
@@ -443,46 +471,42 @@
             total = total + share_in[kind, index].astype(F32)
         return total
 
-    rows = term.shape[3]
-    chunk = ring_out.shape[3]
+    rows = term.shape[2]
+    chunk = ring_out.shape[2]
 
     def start_terms(group, left, right):
-        for index in range(3):
-            product = outer(left[index], right[index]).astype(BF16)
-            for shard in range(feat):
-                term[group, shard, index] = product[shard * rows : (shard + 1) * rows]
+        product = outer(left, right).astype(BF16)
+        for shard in range(feat):
+            term[group, shard] = product[shard * rows : (shard + 1) * rows]
         return [
+            send(term.at[group, f3], pair_in.at[group, 1], pair_sems, (group, 1), feat=f1),
             send(term.at[group, f1], pair_in.at[group, 0], pair_sems, (group, 0), feat=f1),
-            send(term.at[group, f3], pair_in.at[group, 1], pair_sems, (group, 1), feat=f1),
         ]
 
     def cross_terms(group, copies):
         finish(copies)
-        for index in range(3):
-            cross_out[group, index] = (
-                term[group, f2, index].astype(F32) + pair_in[group, 1, index].astype(F32)
-            ).astype(BF16)
+        cross_out[group] = (
+            term[group, f2].astype(F32) + pair_in[group, 1].astype(F32)
+        ).astype(BF16)
         return [send(cross_out.at[group], cross_in.at[group], cross_sems, (group,), feat=f2)]
 
     def ring_terms(group, copies):
         finish(copies)
-        for index in range(3):
-            share = (
-                term[group, f, index].astype(F32)
-                + pair_in[group, 0, index].astype(F32)
-                + cross_in[group, index].astype(F32)
-            ).astype(BF16)
-            for piece in range(dom):
-                ring_out[group, piece, index] = share[piece * chunk : (piece + 1) * chunk]
+        share = (
+            term[group, f].astype(F32)
+            + pair_in[group, 0].astype(F32)
+            + cross_in[group].astype(F32)
+        ).astype(BF16)
+        for piece in range(dom):
+            ring_out[group, piece] = share[piece * chunk : (piece + 1) * chunk]
         return dom_exchange(4 + 2 * group, ring_out.at[group], ring_in.at[group])
 
     def total_terms(group, copies):
         finish(copies)
-        for index in range(3):
-            total = ring_in[group, 0, index].astype(F32)
-            for piece in range(1, dom):
-                total = total + ring_in[group, piece, index].astype(F32)
-            total_buf[group, me, index] = total.astype(BF16)
+        total = ring_in[group, 0].astype(F32)
+        for piece in range(1, dom):
+            total = total + ring_in[group, piece].astype(F32)
+        total_buf[group, me] = total.astype(BF16)
         copies = []
         for step in range(1, dom):
             peer = lax.rem(me + step, dom)
@@ -497,52 +521,62 @@
             )
         return copies
 
-    def write_terms(group, copies, refs):
+    def write_terms(group, copies):
         finish(copies)
-        for index, ref in enumerate(refs):
-            for piece in range(dom):
-                ref[piece * chunk : (piece + 1) * chunk] = factor * total_buf[
-                    group, piece, index
-                ].astype(F32)
-
-    proc_pair = start_terms(0, (src_rows, dst_rows, hidden_p), (grad_p, grad_p, mid_p))
+        for piece in range(dom):
+            terms_ref[group, piece * chunk : (piece + 1) * chunk] = total_buf[group, piece]
+
+    pairs = {
+        3: start_terms(3, src_rows, grad_p),
+        4: start_terms(4, dst_rows, grad_p),
+        5: start_terms(5, hidden_p, mid_p),
+    }
     finish(back_copies)
     g_local = g_local + outer(halo_hot, get_slabs(halo_bin))
     stages = feat_sum(1, g_local)
     next(stages)
     next(stages)
     proc_share = scatter_own(0, spread(edge_hot, normed_p))
-    proc_cross = cross_terms(0, proc_pair)
+    crossing = {group: cross_terms(group, pairs[group]) for group in (3, 4, 5)}
     cot_part = all_parts(cot_buf)
     node_grad = next(stages) + cot_part
 
     mid_e = norm_back(normed_e, scaling_e, pick_wide(target_hot, node_grad)).astype(BF16)
+    pairs[2] = start_terms(2, hidden_e, mid_e)
     grad_e = (matmul_t(mid_e, whole(2)) * slope_e).astype(BF16)
-    enc_pair = start_terms(1, (grid_rows, mesh_rows, hidden_e), (grad_e, grad_e, mid_e))
     put_slabs(slot_bout, grad_e.astype(F32))
     slot_copies = dom_exchange(3, slot_bout, slot_bin)
+    pairs[1] = start_terms(1, mesh_rows, grad_e)
+    pairs[0] = start_terms(0, grid_rows, grad_e)
+    crossing[2] = cross_terms(2, pairs[2])
+    crossing[1] = cross_terms(1, pairs[1])
+    crossing[0] = cross_terms(0, pairs[0])
     enc_share = scatter_own(1, spread(target_hot, matmul_t(grad_e, whole(1))))
-    enc_cross = cross_terms(1, enc_pair)
-    proc_ring = ring_terms(0, proc_cross)
-    own_hot = hot_rows(
-        f * own + lax.broadcasted_iota(jnp.int32, (own, 1), 0), part
-    )
+    order = (3, 4, 5, 2, 1, 0)
+    rings = {group: ring_terms(group, crossing[group]) for group in (3, 4, 5)}
+    own_hot = hot_rows(f * own + lax.broadcasted_iota(jnp.int32, (own, 1), 0), part)
     own_grad = pick_wide(own_hot, node_grad)
     own_latent = matmul(own_hot, latent)
     finish(slot_copies)
     slot_rows = outer(send_hot, get_slabs(slot_bin)).astype(BF16)
     ggrid_ref[...] = matmul_t(slot_rows, whole(0)).astype(BF16)
+    totals = {}
+    totals[3] = total_terms(3, rings[3])
+    rings[2] = ring_terms(2, crossing[2])
+    totals[4] = total_terms(4, rings[4])
+    rings[1] = ring_terms(1, crossing[1])
+    totals[5] = total_terms(5, rings[5])
+    rings[0] = ring_terms(0, crossing[0])
     finish(proc_share)
     out_ref[...] = (own_latent + own_sum(0)).astype(BF16)
-    proc_total = total_terms(0, proc_ring)
-    enc_ring = ring_terms(1, enc_cross)
     finish(enc_share)
     gmesh_ref[...] = (own_grad + own_sum(1)).astype(BF16)
-    enc_total = total_terms(1, enc_ring)
-    write_terms(0, proc_total, (o_ws, o_wd, o_wp))
-    write_terms(1, enc_total, (o_wg, o_wm, o_we))
-    for copies in (across, beside, passed):
-        for copy in copies:
+    for group in (2, 1, 0):
+        totals[group] = total_terms(group, rings[group])
+    for group in order:
+        write_terms(group, totals[group])
+    for copies in (across, beside, passed, sideways, closing):
+        for copy in copies.values():
             copy.wait_send()
 
 
@@ -579,17 +613,17 @@
     indices = jnp.concatenate([slabs(enc_send), slabs(enc_dst), slabs(hal_send), moved, proc_dst])
     slab = pltpu.VMEM((dom, SLAB, width), BF16)
     vmem = pl.BlockSpec(memory_space=pltpu.VMEM)
-    weight_out = jax.ShapeDtypeStruct((shard, width), F32)
-    return pl.pallas_call(
+    factor = 1.0 / math.sqrt(own * dom * feat)
+    out, g_grid, g_mesh, totals = pl.pallas_call(
         functools.partial(fused_kernel, (dom, feat, own, part, edges)),
         out_shape=(
             jax.ShapeDtypeStruct((own, width), BF16),
             jax.ShapeDtypeStruct(grid_feat.shape, BF16),
             jax.ShapeDtypeStruct((own, width), BF16),
         )
-        + (weight_out,) * 6,
+        + (jax.ShapeDtypeStruct((6, shard, width), BF16),),
         in_specs=[vmem] * 10,
-        out_specs=(vmem,) * 9,
+        out_specs=(vmem,) * 4,
         scratch_shapes=[
             pltpu.VMEM((6, feat, shard, width), BF16),
             pltpu.VMEM((feat, own, width), BF16),
@@ -605,19 +639,19 @@
             pltpu.VMEM((2, 4, part, width), BF16),
             pltpu.VMEM((2, feat, own, width), BF16),
             pltpu.VMEM((2, feat, own, width), BF16),
-            pltpu.VMEM((2, feat, 3, shard, width), BF16),
-            pltpu.VMEM((2, 2, 3, shard, width), BF16),
-            pltpu.VMEM((2, 3, shard, width), BF16),
-            pltpu.VMEM((2, 3, shard, width), BF16),
-            pltpu.VMEM((2, dom, 3, chunk, width), BF16),
-            pltpu.VMEM((2, dom, 3, chunk, width), BF16),
-            pltpu.VMEM((2, dom, 3, chunk, width), BF16),
-            pltpu.SemaphoreType.DMA((2, 3, 8)),
-            pltpu.SemaphoreType.DMA((2, 8, dom)),
+            pltpu.VMEM((6, feat, shard, width), BF16),
+            pltpu.VMEM((6, 2, shard, width), BF16),
+            pltpu.VMEM((6, shard, width), BF16),
+            pltpu.VMEM((6, shard, width), BF16),
+            pltpu.VMEM((6, dom, chunk, width), BF16),
+            pltpu.VMEM((6, dom, chunk, width), BF16),
+            pltpu.VMEM((6, dom, chunk, width), BF16),
+            pltpu.SemaphoreType.DMA((2, 5, 8)),
+            pltpu.SemaphoreType.DMA((2, 16, dom)),
             pltpu.SemaphoreType.DMA((2, 2, 2)),
             pltpu.SemaphoreType.DMA((2, 2, feat)),
-            pltpu.SemaphoreType.DMA((2, 2, 2)),
-            pltpu.SemaphoreType.DMA((2, 2)),
+            pltpu.SemaphoreType.DMA((2, 6, 2)),
+            pltpu.SemaphoreType.DMA((2, 6)),
         ],
         compiler_params=pltpu.CompilerParams(
             collective_id=0, has_side_effects=True, vmem_limit_bytes=56 * 1024 * 1024
@@ -635,6 +669,7 @@
         indices[:, None],
         cotangent,
     )
+    return (out, g_grid, g_mesh) + tuple(factor * totals[index].astype(F32) for index in range(6))
 
 
 def choose(*args):
@@ -642,7 +677,7 @@
     feat = lax.axis_size("feat")
     shard = args[2].shape[0]
     fits = max(args[8].shape[1], args[10].shape[1]) <= SLAB
-    if feat == 4 and shard % (dom * TILE) == 0 and fits:
+    if feat == 4 and dom % 2 == 0 and shard % (dom * TILE) == 0 and fits:
         return fused(*args)
     return per_device(*args)
 

time: 118 us -> 100 us (0.85)
  Pallas kernels: 103 us -> 90.8 us
  local copies, waits for them, and re-layouts: 13.1 us -> 5.29 us
  other arithmetic: 0.7 us -> 3.12 us
    pallas_call x1, Pallas kernels: 103 us -> 90.8 us  [fused(): pl.pallas_call(functools.partial(fused_kernel, (dom, feat, own, part, edg...]
    unnamed x34 -> x20, local copies, waits for them, and re-layouts: 11.9 us -> 4.09 us
    mul x0 -> x1, other arithmetic: none -> 2.42 us  [fused(): factor * totals[index].astype(F32)]
where the time goes in v2:
time: 100 us; the launch traced here: 99.9 us
  Pallas kernels  90.8 us (91%)
  local copies, waits for them, and re-layouts  5.29 us (5%)
  other arithmetic  3.12 us (3%)
    pallas_call x1, Pallas kernels, fused(): pl.pallas_call(functools.partial(fused_kernel, (dom, feat, own, part, edg...  90.8 us
    unnamed x20, local copies, waits for them, and re-layouts  4.09 us
    mul x1, other arithmetic, fused(): factor * totals[index].astype(F32)  2.42 us

profile of v2, /device:TPU:0, one launch (start us, length us, event | category | flops | bytes accessed | tf_op | source)
XLA Modules:
  0.0 99.9 jit_solution(7242041638666868366)
XLA Ops:
  0.6 0.0 copy-start.4
  0.7 0.7 fusion.1
  1.4 0.0 copy-done.4
  1.4 0.1 copy.30
  1.4 0.0 copy-start.5
  1.5 0.1 reshape.45
  1.5 0.6 copy-done.5
  2.1 0.1 copy.31
  2.2 0.0 copy-start.3
  2.2 0.1 reshape.46
  2.3 0.6 copy-done.3
  2.9 0.1 copy.32
  3.0 0.0 copy-start.6
  3.0 0.1 reshape.47
  3.1 0.6 copy-done.6
  3.7 0.1 concatenate.3
  3.7 0.9 copy.29.index_ref
  4.6 90.8 %fused_layer.1 = (bf16[40,512]{1,0:T(8,128)(2,1)}, bf16[512,512]{1,0:T(8,128)(2,1)}, bf16[40,512]{1,0:T(8,128)(2,1)}, bf16[6,128,512]{2,1,0:T(8,128)(2,1)}) custom-call(bf16[512,512]{1,0:T(8,128)(2,1)} %grid_ref.1, bf16[40,512]{1,0:T(8,128)(2,1)} %mesh_ref.1, bf16[128,512]{1,0:T(8,128)(2,1)} %wg_ref.1, bf16[128,512]{1,0:T(8,128)(2,1)} %wm_ref.1, ...), custom_call_target="tpu_custom_call" | custom-call | tf_op jit(solution)/shard_map/fused_layer/pallas_call | solution.py:617
  95.4 0.0 copy-start.2
  95.4 0.0 copy-start
  95.5 2.4 %multiply_bitcast_fusion = (f32[128,512]{1,0:T(8,128)}, f32[128,512]{1,0:T(8,128)}, f32[128,512]{1,0:T(8,128)}, f32[128,512]{1,0:T(8,128)}, f32[128,512]{1,0:T(8,128)}, /*index=5*/f32[128,512]{1,0:T(8,128)}) fusion(bf16[6,128,512]{2,1,0:T(8,128)(2,1)} %get-tuple-element.16), kind=kLoop, calls=%fused_computation | loop fusion | flops 786432 | bytes 2359296 | tf_op jit(solution)/shard_map/mul | solution.py:672
  97.9 0.0 copy-done.2
  97.9 0.6 copy.36
  98.5 0.0 copy-done
  98.5 0.0 copy-start.1
  98.5 0.8 copy.37
  99.3 0.0 copy-done.1
  99.3 0.6 copy.38
  (3 shorter events, 0.0 us)
Async XLA Ops:
  0.6 0.7 copy-start.4
  1.4 0.7 copy-start.5
  2.2 0.7 copy-start.3
  3.0 0.7 copy-start.6
  95.4 2.4 %copy-start.2 = (bf16[40,512]{1,0:T(8,128)(2,1)S(1)}, bf16[40,512]{1,0:T(8,128)(2,1)}, u32[]{:S(2)}) copy-start(bf16[40,512]{1,0:T(8,128)(2,1)} %get-tuple-element.32) | copy-start | bytes 122884
  95.4 3.1 %copy-start = (bf16[512,512]{1,0:T(8,128)(2,1)S(1)}, bf16[512,512]{1,0:T(8,128)(2,1)}, u32[]{:S(2)}) copy-start(bf16[512,512]{1,0:T(8,128)(2,1)} %get-tuple-element.33) | copy-start | bytes 1572868
  98.5 0.8 copy-start.1
